TPU v7x, 256 devices: a whole 4x4x8 slice. The times are simulated.
256 devices in a mesh: ep: 64 (over z, x, core), tp: 4 (over y).
Axes of the slice: x: 4, y: 4, z: 8, core: 2. Of those that a mesh axis runs over, the one named last changes fastest.
Arguments:
- tokens: bfloat16 [16384, 2048], P('ep', 'tp'), may hold values from -180 to 180
- norm_gain: float32 [2048], replicated, may hold values from 0.1 to 1.9
- router_weight: bfloat16 [2048, 60], P('tp'), may hold values from -2 to 2
- shared_gate_w: bfloat16 [2048], replicated, may hold values from -0.125 to 0.125
- expert_ids: int32 [16384, 4], P('ep'), may hold values from 0 to 59, all different within a row; in each aligned block of 256 rows (0 to 255, 256 to 511, ...) at most 32 rows name the same one
- w_gate: bfloat16 [64, 2048, 1408], P('ep', None, 'tp'), may hold values from -0.125 to 0.125
- w_up: bfloat16 [64, 2048, 1408], P('ep', None, 'tp'), may hold values from -0.125 to 0.125
- w_down: bfloat16 [64, 1408, 2048], P('ep', 'tp'), may hold values from -1.5 to 1.5
- shared_w_gate: bfloat16 [2048, 2816], P(None, 'tp'), may hold values from -0.125 to 0.125
- shared_w_up: bfloat16 [2048, 2816], P(None, 'tp'), may hold values from -0.125 to 0.125
- shared_w_down: bfloat16 [2816, 2048], P('tp'), may hold values from -0.109375 to 0.109375
Outputs:
- moe_out: bfloat16 [16384, 2048], P('ep', 'tp')
Inputs may be any that keep to these rules, and one draw needn't show every extreme that they name: `expert_ids`: each row names 4 different experts below 60. Within the 256 rows of one index of ep no expert is named by more than 32 rows, and in some of these blocks one expert is named by exactly 32 rows.
All inputs are finite; a program needn't handle non-finite values.
Results may differ from a plain program's by a relative error of at most 0.0069.
Values may be sent and summed in bfloat16 or wider, within the bound.
No kernel may reach another device: no remote copies, remote signals or barrier semaphores. Data moves between devices by JAX's collectives and lax.ppermute only.
A program may use at most 128 MiB of HBM per device.

v0:
```python
import jax
import jax.numpy as jnp
from jax import lax
from jax.sharding import PartitionSpec as P


def laid_out(parts, dim):
    lengths = list(parts.shape[1:])
    lengths[dim] *= parts.shape[0]
    return jnp.moveaxis(parts, 0, dim).reshape(lengths)


def copy_for_each(value, axis):
    peers = lax.axis_size(axis)
    return lax.all_to_all(
        jnp.broadcast_to(value[None], (peers, *value.shape)), axis, 0, 0, tiled=True
    )


def collect(value, axis, dim):
    return laid_out(copy_for_each(value, axis), dim)


def taken_together(value, axis):
    return copy_for_each(value, axis).sum(axis=0)


def turned_gather(arrays, axis, dims):
    turned = [jnp.moveaxis(a, dim, 0) for a, dim in zip(arrays, dims)]
    both = jnp.concatenate([t.reshape(len(t), -1) for t in turned], axis=1)
    out, at, done = (lax.all_gather(both, axis, axis=0, tiled=True), 0, [])
    for t, dim in zip(turned, dims):
        piece = out[:, at : at + t[0].size].reshape(-1, *t.shape[1:])
        done.append(jnp.moveaxis(piece, 0, dim))
        at += t[0].size
    return tuple(done)


def cut_along(value, dim, peers):
    before, after = (value.shape[:dim], value.shape[dim + 1 :])
    return jnp.moveaxis(value.reshape(*before, peers, -1, *after), dim, 0)


def sent_and_summed(value, axis, dim):
    peers = lax.axis_size(axis)
    parts = lax.all_to_all(cut_along(value, dim, peers), axis, 0, 0, tiled=True)
    return jnp.sum(parts.astype(jnp.float32), axis=0)


def send_back(summed):
    return lax.all_to_all(summed, "ep", split_axis=0, concat_axis=0, tiled=True)


def expert_rows(arrived, w_gate, w_up, w_down):
    share = arrived.shape[0] // lax.axis_size("tp")
    mine = lax.dynamic_slice_in_dim(arrived, lax.axis_index("tp") * share, share, 0)
    gate_act = jnp.einsum("sekd,edf->sekf", mine, w_gate, preferred_element_type=jnp.float32)
    up_act = jnp.einsum("sekd,edf->sekf", mine, w_up, preferred_element_type=jnp.float32)
    hidden = (jax.nn.silu(gate_act) * up_act).astype(jnp.bfloat16)
    full_out = jnp.einsum(
        "sekf,efd->sekd", hidden, w_down, preferred_element_type=jnp.float32
    ).astype(jnp.bfloat16)
    summed = lax.all_to_all(full_out, "tp", split_axis=3, concat_axis=0, tiled=True)
    return send_back(summed)


def per_device(
    tokens,
    norm_gain,
    router_weight,
    shared_gate_w,
    expert_ids,
    w_gate,
    w_up,
    w_down,
    shared_w_gate,
    shared_w_up,
    shared_w_down,
):
    width = tokens.shape[1]
    tok_rows = tokens.shape[0]
    column_start = lax.axis_index("tp") * width
    whole = collect(tokens, "tp", 1)
    values = whole.astype(jnp.float32)
    inv_rms = lax.rsqrt(jnp.mean(values * values, axis=-1, keepdims=True) + 1e-06)
    normed = (values * inv_rms * norm_gain[None, :]).astype(jnp.bfloat16)
    own_part = lax.dynamic_slice_in_dim(normed, column_start, width, 1)
    partial_logits = jnp.dot(own_part, router_weight, preferred_element_type=jnp.float32)
    logits = taken_together(partial_logits, "tp")
    probs = jax.nn.softmax(logits, axis=-1)
    expert_count = logits.shape[1]
    matches = expert_ids[:, :, None] == jnp.arange(expert_count, dtype=jnp.int32)[None, None, :]
    route_weight = jnp.sum(jnp.where(matches, probs[:, None, :], 0.0), axis=-1)
    gate_whole, up_whole = turned_gather((w_gate, w_up), "tp", (2, 2))
    down_whole = lax.all_gather(w_down, "tp", axis=1, tiled=True)
    experts_here = w_gate.shape[0]
    slot_count = lax.axis_size("ep") * experts_here
    capacity = tok_rows // 8
    flat_ids = expert_ids.reshape(-1)
    one_hot = (flat_ids[:, None] == jnp.arange(slot_count, dtype=jnp.int32)[None, :]).astype(
        jnp.int32
    )
    before = jnp.cumsum(one_hot, axis=0) - one_hot
    order_rank = jnp.sum(before * one_hot, axis=1)
    slot_ids = (flat_ids * capacity + order_rank).reshape(expert_ids.shape)
    targets = jnp.arange(slot_count * capacity, dtype=jnp.int32)
    dispatch_map = jnp.sum(
        (slot_ids[None, :, :] == targets[:, None, None]).astype(jnp.bfloat16), axis=2
    )
    outgoing = jnp.dot(dispatch_map, normed, preferred_element_type=jnp.float32).astype(
        jnp.bfloat16
    )
    outgoing = outgoing.reshape(lax.axis_size("ep"), experts_here, capacity, normed.shape[1])
    returned = expert_rows(
        lax.all_to_all(outgoing, "ep", split_axis=0, concat_axis=0, tiled=True),
        w_gate=gate_whole,
        w_up=up_whole,
        w_down=down_whole,
    )
    picked = returned.reshape(slot_count * capacity, width)[slot_ids]
    routed = jnp.sum(route_weight[:, :, None] * picked.astype(jnp.float32), axis=1)
    shared_gate_act = jnp.dot(normed, shared_w_gate, preferred_element_type=jnp.float32)
    shared_up_act = jnp.dot(normed, shared_w_up, preferred_element_type=jnp.float32)
    shared_hidden = (jax.nn.silu(shared_gate_act) * shared_up_act).astype(jnp.bfloat16)
    shared_part = jnp.dot(shared_hidden, shared_w_down, preferred_element_type=jnp.float32)
    shared_own = sent_and_summed(shared_part.astype(jnp.bfloat16), "tp", 1)
    share_gate = jax.nn.sigmoid(jnp.dot(normed, shared_gate_w, preferred_element_type=jnp.float32))
    return (share_gate[:, None] * shared_own + routed).astype(jnp.bfloat16)


def solution(mesh):
    return jax.shard_map(
        per_device,
        mesh=mesh,
        in_specs=(
            P("ep", "tp"),
            P(),
            P("tp", None),
            P(),
            P("ep", None),
            P("ep", None, "tp"),
            P("ep", None, "tp"),
            P("ep", "tp", None),
            P(None, "tp"),
            P(None, "tp"),
            P("tp", None),
        ),
        out_specs=P("ep", "tp"),
        check_vma=False,
    )
```

profile of v0, /device:TPU:8, one launch (start us, length us, event | category | flops | bytes accessed | tf_op | source)
XLA Modules:
  0.0 429.5 jit_solution(3899483268526843282)
XLA Ops:
  6.5 3.8 pad_maximum_fusion
  10.4 0.9 copy-done.3
  11.3 0.1 copy.93
  11.4 1.0 broadcast_in_dim.14
  12.5 6.4 %all-to-all-start = ((bf16[4,256,512]{1,2,0:T(8,128)(2,1)}), bf16[4,256,512]{1,2,0:T(8,128)(2,1)}, u32[]{:S(2)}, u32[]{:S(2)}) async-start(bf16[4,256,512]{1,2,0:T(8,128)(2,1)} %broadcast_in_dim.14), calls=%async_computation | async-start | bytes 2097152 | tf_op jit(solution)/shard_map/all_to_all | solution.py:15
  18.8 0.1 copy.97
  19.2 18.0 %reduce-window.6 = s32[64,8,128]{2,1,0:T(8,128)S(1)} reduce-window(s32[64,8,128]{2,1,0:T(8,128)S(1)} %fusion.47, s32[]{:T(128)} %constant.8.clone.1), window={size=1x1x128 pad=0_0x0_0x127_0}, to_apply=%region_6.7 | reduce-window | flops 8323072 | bytes 524292 | tf_op jit(solution)/shard_map/reduce-window
  37.3 0.1 slice.19
  37.4 0.1 copy.99
  37.7 0.1 broadcast_add_fusion
  37.9 0.1 reduce_sum.83
  38.1 2.5 fusion.7
  40.7 1.6 multiply_reduce_fusion.1
  42.3 1.6 fusion.32
  43.9 5.8 %convolution_convert_fusion = bf16[2048,2048]{1,0:T(8,128)(2,1)} fusion(bf16[2048,256]{1,0:T(8,128)(2,1)S(1)} %copy-done.2, bf16[256,2048]{0,1:T(8,128)(2,1)S(1)} %fusion.32), kind=kOutput, calls=%fused_computation.3 | convolution fusion | flops 2151677952 | bytes 10485760 | tf_op jit(solution)/shard_map/dot_general | solution.py:110
  49.7 10.9 %all-to-all-start.3 = ((bf16[64,1,32,2048]{3,2,1,0:T(8,128)(2,1)}), bf16[64,1,32,2048]{3,2,1,0:T(8,128)(2,1)}, u32[]{:S(2)}, u32[]{:S(2)}) async-start(bf16[64,1,32,2048]{3,2,1,0:T(8,128)(2,1)} %bitcast.131), calls=%async_computation.3 | async-start | bytes 16777216 | tf_op jit(solution)/shard_map/all_to_all | solution.py:115
  60.6 0.7 all-gather.5.cloned.1.call-update
  61.4 1.1 fusion.45
  62.5 63.2 %all-gather.3.cloned.1.call-done = bf16[1408,4096]{1,0:T(8,128)(2,1)} async-done(((bf16[352,4096]{1,0:T(8,128)(2,1)}), bf16[1408,4096]{1,0:T(8,128)(2,1)}) %all-gather.3.cloned.1.call-update) | async-done | bytes 11534352 | tf_op jit(solution)/shard_map/all_gather | solution.py:31
  125.7 11.0 %fusion.56 = (bf16[1408,2048]{1,0:T(8,128)(2,1)}, bf16[1408,2048]{1,0:T(8,128)(2,1)}) fusion(bf16[1408,4096]{1,0:T(8,128)(2,1)} %all-gather.3.cloned.1.call-done), kind=kLoop, calls=%fused_computation.61 | loop fusion | bytes 23068672 | tf_op jit(solution)/shard_map/slice | solution.py:33
  136.6 8.5 %copy.110 = bf16[1408,2048]{0,1:T(8,128)(2,1)} copy(bf16[1408,2048]{1,0:T(8,128)(2,1)} %get-tuple-element.7) | data formatting | bytes 11534336
  145.2 8.4 %copy.111 = bf16[1408,2048]{0,1:T(8,128)(2,1)} copy(bf16[1408,2048]{1,0:T(8,128)(2,1)} %get-tuple-element.8) | data formatting | bytes 11534336
  153.5 93.2 %all-to-all-done.3 = bf16[64,1,32,2048]{3,2,1,0:T(8,128)(2,1)} async-done(((bf16[64,1,32,2048]{3,2,1,0:T(8,128)(2,1)}), bf16[64,1,32,2048]{3,2,1,0:T(8,128)(2,1)}, u32[]{:S(2)}, u32[]{:S(2)}) %all-to-all-start.3) | async-done | bytes 8388640 | tf_op jit(solution)/shard_map/all_to_all | solution.py:115
  246.8 0.7 broadcast_in_dim.15
  247.5 4.8 %all-to-all-start.2 = ((f32[4,256,60]{1,2,0:T(8,128)}), f32[4,256,60]{1,2,0:T(8,128)S(1)}, u32[]{:S(2)}, u32[]{:S(2)}) async-start(f32[4,256,60]{1,2,0:T(8,128)} %broadcast_in_dim.15), calls=%async_computation.2 | async-start | bytes 524288 | tf_op jit(solution)/shard_map/all_to_all | solution.py:15
  252.3 8.3 %fusion.8 = f32[16,1,32,1408]{3,2,0,1:T(8,128)} fusion(bf16[1408,2048]{0,1:T(8,128)(2,1)} %copy.110, bf16[64,1,32,2048]{3,2,1,0:T(8,128)(2,1)} %all-to-all-done.3, s32[]{:T(128)S(6)} %select_n.15), kind=kOutput, calls=%fused_computation.11 | convolution fusion | flops 2952790016 | bytes 10747908 | tf_op jit(solution)/shard_map/sekd,edf->sekf/dot_general | solution.py:57
  260.6 14.2 %fusion.23 = bf16[16,1,32,2048]{3,2,0,1:T(8,128)(2,1)} fusion(bf16[1,1408,2048]{2,1,0:T(8,128)(2,1)} %all-gather.5.cloned.1.call-done, bf16[1408,2048]{0,1:T(8,128)(2,1)} %copy.111, f32[16,1,32,1408]{3,2,0,1:T(8,128)} %fusion.8, bf16[64,1,32,2048]{3,2,1,0:T(8,128)(2,1)} %all-to-all-done.3, s32[]{:T(128)S(6)} %select_n.15), kind=kOutput, calls=%fused_computation.17 | convolution fusion | flops 5910953984 | bytes 18612228 | tf_op jit(solution)/shard_map/sekf,efd->sekd/dot_general | solution.py:60
  274.8 9.9 %copy.104 = bf16[16,1,32,2048]{2,0,1,3:T(8,128)(2,1)} copy(bf16[16,1,32,2048]{3,2,0,1:T(8,128)(2,1)} %fusion.23) | data formatting | bytes 4194304 | tf_op jit(solution)/shard_map/convert_element_type | solution.py:62
  284.7 10.6 %reshape.141 = bf16[4,2,131072]{2,1,0:T(2,128)(2,1)} reshape(bf16[2048,1,16,32]{3,2,1,0:T(8,128)(2,1)} %bitcast.132) | data formatting | bytes 4194304
  295.3 4.8 %all-to-all-start.4 = ((bf16[4,2,131072]{2,1,0:T(2,128)(2,1)}), bf16[4,2,131072]{2,1,0:T(2,128)(2,1)}, u32[]{:S(2)}, u32[]{:S(2)}) async-start(bf16[4,2,131072]{2,1,0:T(2,128)(2,1)} %reshape.141), calls=%async_computation.4 | async-start | bytes 4194304 | tf_op jit(solution)/shard_map/all_to_all | solution.py:63
  300.1 3.9 fusion.58
  304.0 6.5 %convolution_convert_fusion.1 = bf16[256,2048]{1,0:T(8,128)(2,1)} fusion(bf16[704,2048]{1,0:T(8,128)(2,1)S(1)} %copy-done, bf16[2048,704]{0,1:T(8,128)(2,1)} %param.20, bf16[256,2048]{0,1:T(8,128)(2,1)} %copy-done.1, f32[256,704]{0,1:T(8,128)} %fusion.58), kind=kOutput, calls=%fused_computation.19 | convolution fusion | flops 1478000640 | bytes 8585216 | tf_op jit(solution)/shard_map/dot_general | solution.py:125
  310.5 2.4 copy.116
  312.9 8.3 %all-to-all-done.4 = bf16[4,2,131072]{2,1,0:T(2,128)(2,1)} async-done(((bf16[4,2,131072]{2,1,0:T(2,128)(2,1)}), bf16[4,2,131072]{2,1,0:T(2,128)(2,1)}, u32[]{:S(2)}, u32[]{:S(2)}) %all-to-all-start.4) | async-done | bytes 2097184 | tf_op jit(solution)/shard_map/all_to_all | solution.py:63
  321.1 5.7 %all-to-all-start.1 = ((bf16[4,256,512]{2,1,0:T(8,128)(2,1)}), bf16[4,256,512]{2,1,0:T(8,128)(2,1)}, u32[]{:S(2)}, u32[]{:S(2)}) async-start(bf16[4,256,512]{2,1,0:T(8,128)(2,1)} %bitcast.136), calls=%async_computation.1 | async-start | bytes 2097152 | tf_op jit(solution)/shard_map/all_to_all | solution.py:46
  326.8 7.4 %reshape.142 = bf16[2048,1,16,32]{3,2,1,0:T(8,128)(2,1)} reshape(bf16[4,2,131072]{2,1,0:T(2,128)(2,1)} %all-to-all-done.4) | data formatting | bytes 4194304
  334.2 9.9 %copy.109 = bf16[16,1,32,4,512]{4,3,2,0,1:T(4,128)(2,1)} copy(bf16[16,1,32,4,512]{2,0,4,3,1:T(8,128)(2,1)} %bitcast.133) | data formatting | bytes 4194304 | tf_op jit(solution)/shard_map/all_to_all | solution.py:63
  344.1 3.4 copy.106
  347.6 10.4 %all-to-all-start.5 = ((bf16[64,1,32,512]{3,2,1,0:T(8,128)(2,1)}), bf16[64,1,32,512]{3,2,1,0:T(8,128)(2,1)}, u32[]{:S(2)}, u32[]{:S(2)}) async-start(bf16[64,1,32,512]{3,2,1,0:T(8,128)(2,1)} %bitcast.135), calls=%async_computation.5 | async-start | bytes 4194304 | tf_op jit(solution)/shard_map/all_to_all | solution.py:51
  358.0 0.1 copy.108
  358.3 1.5 fusion.57
  360.0 0.1 copy.95
  360.1 1.5 convert_reduce_fusion
  361.6 47.6 %all-to-all-done.5 = bf16[64,1,32,512]{3,2,1,0:T(8,128)(2,1)} async-done(((bf16[64,1,32,512]{3,2,1,0:T(8,128)(2,1)}), bf16[64,1,32,512]{3,2,1,0:T(8,128)(2,1)}, u32[]{:S(2)}, u32[]{:S(2)}) %all-to-all-start.5) | async-done | bytes 2097184 | tf_op jit(solution)/shard_map/all_to_all | solution.py:51
  409.1 7.0 %gather_fusion = bf16[1024,512]{1,0:T(8,128)(2,1)} fusion(bf16[2048,512]{1,0:T(8,128)(2,1)} %bitcast.36, s32[1024]{0:T(1024)S(1)} %broadcast_clamp_fusion), kind=kCustom, calls=%fused_computation | custom fusion | bytes 2101248 | tf_op jit(solution)/shard_map/gather | solution.py:120
  416.1 2.8 reshape.135
  418.8 3.0 multiply_reduce_fusion
  421.8 0.8 add_convert_fusion
  (41 shorter events, 1.0 us)
Async XLA Ops:
  6.5 297.4 %copy-start = (bf16[704,2048]{1,0:T(8,128)(2,1)S(1)}, bf16[704,2048]{1,0:T(8,128)(2,1)}, u32[]{:S(2)}) copy-start(bf16[704,2048]{1,0:T(8,128)(2,1)} %param.21) | copy-start | bytes 8650756
  6.5 119.1 %all-gather.3.cloned.1.call-start = ((), (), s32[]{:S(2)}) async-start(), calls=%async_computation.6 | async-start | bytes 14417920 | tf_op jit(solution)/shard_map/all_gather | solution.py:31
  10.3 0.9 copy-start.3
  10.4 8.5 %copy-start.5 = (s32[256,4]{0,1:T(4,128)S(1)}, s32[256,4]{0,1:T(4,128)}, u32[]{:S(2)}) copy-start(s32[256,4]{0,1:T(4,128)} %param.15) | copy-start | bytes 12292
  12.5 28.2 %all-to-all-start = ((bf16[4,256,512]{1,2,0:T(8,128)(2,1)}), bf16[4,256,512]{1,2,0:T(8,128)(2,1)}, u32[]{:S(2)}, u32[]{:S(2)}) async-start(bf16[4,256,512]{1,2,0:T(8,128)(2,1)} %broadcast_in_dim.14), calls=%async_computation | async-start | bytes 2097152 | tf_op jit(solution)/shard_map/all_to_all | solution.py:15
  18.8 23.5 %copy-start.6 = (f32[2048]{0:T(1024)S(1)}, f32[2048]{0:T(1024)}, u32[]{:S(2)}) copy-start(f32[2048]{0:T(1024)} %param.12) | copy-start | bytes 24580
  40.7 3.2 copy-start.2
  43.9 5.8 %copy-start.1 = (bf16[256,2048]{0,1:T(8,128)(2,1)}, bf16[256,2048]{0,1:T(8,128)(2,1)S(1)}, u32[]{:S(2)}) copy-start(bf16[256,2048]{0,1:T(8,128)(2,1)S(1)} %fusion.32) | copy-start | bytes 3145732
  49.7 11.7 %copy-start.4 = (bf16[512,60]{0,1:T(8,128)(2,1)S(1)}, bf16[512,60]{0,1:T(8,128)(2,1)}, u32[]{:S(2)}) copy-start(bf16[512,60]{0,1:T(8,128)(2,1)} %param.13) | copy-start | bytes 184324
  49.7 197.1 %all-to-all-start.3 = ((bf16[64,1,32,2048]{3,2,1,0:T(8,128)(2,1)}), bf16[64,1,32,2048]{3,2,1,0:T(8,128)(2,1)}, u32[]{:S(2)}, u32[]{:S(2)}) async-start(bf16[64,1,32,2048]{3,2,1,0:T(8,128)(2,1)} %bitcast.131), calls=%async_computation.3 | async-start | bytes 16777216 | tf_op jit(solution)/shard_map/all_to_all | solution.py:115
  60.6 200.0 %all-gather.5.cloned.1.call-start = ((), (), s32[]{:S(2)}) async-start(), calls=%async_computation.7 | async-start | bytes 7208960 | tf_op jit(solution)/shard_map/all_gather | solution.py:95
  247.5 47.8 %all-to-all-start.2 = ((f32[4,256,60]{1,2,0:T(8,128)}), f32[4,256,60]{1,2,0:T(8,128)S(1)}, u32[]{:S(2)}, u32[]{:S(2)}) async-start(f32[4,256,60]{1,2,0:T(8,128)} %broadcast_in_dim.15), calls=%async_computation.2 | async-start | bytes 524288 | tf_op jit(solution)/shard_map/all_to_all | solution.py:15
  295.3 25.9 %all-to-all-start.4 = ((bf16[4,2,131072]{2,1,0:T(2,128)(2,1)}), bf16[4,2,131072]{2,1,0:T(2,128)(2,1)}, u32[]{:S(2)}, u32[]{:S(2)}) async-start(bf16[4,2,131072]{2,1,0:T(2,128)(2,1)} %reshape.141), calls=%async_computation.4 | async-start | bytes 4194304 | tf_op jit(solution)/shard_map/all_to_all | solution.py:63
  321.1 26.4 %all-to-all-start.1 = ((bf16[4,256,512]{2,1,0:T(8,128)(2,1)}), bf16[4,256,512]{2,1,0:T(8,128)(2,1)}, u32[]{:S(2)}, u32[]{:S(2)}) async-start(bf16[4,256,512]{2,1,0:T(8,128)(2,1)} %bitcast.136), calls=%async_computation.1 | async-start | bytes 2097152 | tf_op jit(solution)/shard_map/all_to_all | solution.py:46
  347.6 10.6 %copy-start.7 = (bf16[2048]{0:T(1024)(128)(2,1)S(1)}, bf16[2048]{0:T(1024)(128)(2,1)}, u32[]{:S(2)}) copy-start(bf16[2048]{0:T(1024)(128)(2,1)} %param.14) | copy-start | bytes 12292
  347.6 61.6 %all-to-all-start.5 = ((bf16[64,1,32,512]{3,2,1,0:T(8,128)(2,1)}), bf16[64,1,32,512]{3,2,1,0:T(8,128)(2,1)}, u32[]{:S(2)}, u32[]{:S(2)}) async-start(bf16[64,1,32,512]{3,2,1,0:T(8,128)(2,1)} %bitcast.135), calls=%async_computation.5 | async-start | bytes 4194304 | tf_op jit(solution)/shard_map/all_to_all | solution.py:51
Sparse Core Ops, SparseCore 0:
  10.5 115.1 all-gather.2
  127.5 64.4 all-gather.4
where the time goes:
time: 431 us; the launch traced here: 429 us
  waiting for transfers between devices  213 us (49%)
  local copies, waits for them, and re-layouts  85.4 us (20%)
  starting transfers between devices  42.9 us (10%)
  matrix products  41.3 us (10%)
  other arithmetic  33.3 us (8%)
  between operations  13.6 us (3%)
    all_to_all x1, waiting for transfers between devices, per_device(): lax.all_to_all(outgoing, 'ep', split_axis=0, concat_axis=0, tiled=True)  93.2 us
    all_gather x1, waiting for transfers between devices, turned_gather(): out, at, done = (lax.all_gather(both, axis, axis=0, tiled=True), 0, [])  63.2 us
    all_to_all x1, waiting for transfers between devices, send_back(): return lax.all_to_all(summed, 'ep', split_axis=0, concat_axis=0, tiled=True)  47.6 us
    unnamed x23, local copies, waits for them, and re-layouts  36.1 us
    another operation x3, other arithmetic  18.2 us
    dot_general x1, matrix products, expert_rows(): jnp.einsum('sekf,efd->sekd', hidden, w_down, preferred_element_type=jnp.f...  14.2 us
    all_to_all x2, local copies, waits for them, and re-layouts, expert_rows(): lax.all_to_all(full_out, 'tp', split_axis=3, concat_axis=0, tiled=True)  13.4 us
    all_to_all x2, starting transfers between devices, copy_for_each(): lax.all_to_all(jnp.broadcast_to(value[None], (peers, *value.shape)), axis...  11.2 us
  transfers between devices with their start and end apart: 8, of which 4 were waited for; matrix products, arithmetic and copies ran while one was open for 33% of the time, Pallas kernels for 0%

commit v1 on v0

--- a/solution.py
+++ b/solution.py
@@ -1,7 +1,40 @@
+import functools
 import jax
 import jax.numpy as jnp
 from jax import lax
 from jax.sharding import PartitionSpec as P
+
+
+def prepare_set(x_in, axis_k, a0):
+    newest, y_new = (x_in.shape[:axis_k], x_in.shape[axis_k + 1 :])
+    found_now = jnp.moveaxis(x_in.reshape(*newest, a0, -1, *y_new), axis_k, 0)
+    return found_now
+
+
+def bind_samples_for(load, which_dim):
+    front = list(load.shape[1:])
+    front[which_dim] *= load.shape[0]
+    tall = jnp.moveaxis(load, 0, which_dim).reshape(front)
+    return tall
+
+
+def expand_matrix(local_x, net_axis, block_in, v0):
+    h_now, fresh = (lax.axis_size(net_axis), lax.axis_index(net_axis))
+    current_value = prepare_set(local_x, block_in, h_now)
+    pile = [current_value[fresh]]
+    for to_i in range(1, h_now):
+        placed = current_value[(fresh + to_i) % h_now]
+        pile.append(
+            lax.ppermute(
+                placed, axis_name=net_axis, perm=[(d, (d + to_i) % h_now) for d in range(h_now)]
+            )
+        )
+    current_value = jnp.stack(pile, 0)[(fresh - jnp.arange(h_now)) % h_now]
+    far_arr = bind_samples_for(current_value, v0)
+    return far_arr
+
+
+lay_the_stocks = functools.partial(expand_matrix, net_axis="tp", block_in=3, v0=0)
 
 
 def laid_out(parts, dim):
@@ -60,7 +93,7 @@
     full_out = jnp.einsum(
         "sekf,efd->sekd", hidden, w_down, preferred_element_type=jnp.float32
     ).astype(jnp.bfloat16)
-    summed = lax.all_to_all(full_out, "tp", split_axis=3, concat_axis=0, tiled=True)
+    summed = lay_the_stocks(full_out)
     return send_back(summed)
 
 

time: 431 us -> 401 us (0.930)
  local copies, waits for them, and re-layouts: 85.4 us -> 54.5 us
    ppermute x0 -> x3, waiting for transfers between devices: none -> 21.6 us  [expand_matrix(): lax.ppermute(placed, axis_name=net_axis, perm=[(d, (d + to_i) % h_now) fo...]
    unnamed x23 -> x29, local copies, waits for them, and re-layouts: 36.1 us -> 18.6 us
    all_to_all x2 -> x0, local copies, waits for them, and re-layouts: 13.4 us -> none  [expert_rows(): lax.all_to_all(full_out, 'tp', split_axis=3, concat_axis=0, tiled=True)]
    all_gather x1, waiting for transfers between devices: 63.2 us -> 50.4 us  [turned_gather(): out, at, done = (lax.all_gather(both, axis, axis=0, tiled=True), 0, [])]
    convert_element_type x1 -> x0, local copies, waits for them, and re-layouts: 9.95 us -> none  [expert_rows(): full_out = jnp.einsum('sekf,efd->sekd', hidden, w_down, preferred_element...]
    all_to_all x1 -> x0, waiting for transfers between devices: 8.27 us -> none  [expert_rows(): lax.all_to_all(full_out, 'tp', split_axis=3, concat_axis=0, tiled=True)]
    ppermute x0 -> x3, starting transfers between devices: none -> 5.2 us  [expand_matrix(): lax.ppermute(placed, axis_name=net_axis, perm=[(d, (d + to_i) % h_now) fo...]
    all_to_all x1 -> x0, starting transfers between devices: 4.8 us -> none  [expert_rows(): lax.all_to_all(full_out, 'tp', split_axis=3, concat_axis=0, tiled=True)]
  transfers between devices with their start and end apart: 8 -> 10, of which waited for: 4 -> 5; matrix products, arithmetic and copies ran while one was open for 33% -> 28% of each run, Pallas kernels for 0% -> 0%
where the time goes in v1:
time: 401 us; the launch traced here: 399 us
  waiting for transfers between devices  214 us (53%)
  local copies, waits for them, and re-layouts  54.5 us (14%)
  starting transfers between devices  42.4 us (11%)
  matrix products  40.1 us (10%)
  other arithmetic  33.6 us (8%)
  between operations  13.7 us (3%)
    all_to_all x1, waiting for transfers between devices, per_device(): lax.all_to_all(outgoing, 'ep', split_axis=0, concat_axis=0, tiled=True)  93.1 us
    all_gather x1, waiting for transfers between devices, turned_gather(): out, at, done = (lax.all_gather(both, axis, axis=0, tiled=True), 0, [])  50.4 us
    all_to_all x1, waiting for transfers between devices, send_back(): return lax.all_to_all(summed, 'ep', split_axis=0, concat_axis=0, tiled=True)  48.8 us
    ppermute x3, waiting for transfers between devices, expand_matrix(): lax.ppermute(placed, axis_name=net_axis, perm=[(d, (d + to_i) % h_now) fo...  21.6 us
    unnamed x29, local copies, waits for them, and re-layouts  18.6 us
    another operation x3, other arithmetic  18.2 us
    dot_general x1, matrix products, expert_rows(): jnp.einsum('sekf,efd->sekd', hidden, w_down, preferred_element_type=jnp.f...  14.1 us
    all_to_all x2, starting transfers between devices, copy_for_each(): lax.all_to_all(jnp.broadcast_to(value[None], (peers, *value.shape)), axis...  11.2 us
  transfers between devices with their start and end apart: 10, of which 5 were waited for; matrix products, arithmetic and copies ran while one was open for 28% of the time, Pallas kernels for 0%

profile of v1, /device:TPU:8, one launch (start us, length us, event | category | flops | bytes accessed | tf_op | source)
XLA Modules:
  0.0 398.7 jit_solution(4577122277651311465)
XLA Ops:
  6.5 3.8 pad_maximum_fusion
  10.4 0.9 copy-done.5
  11.4 1.0 broadcast_in_dim.14
  12.5 6.4 %all-to-all-start = ((bf16[4,256,512]{1,2,0:T(8,128)(2,1)}), bf16[4,256,512]{1,2,0:T(8,128)(2,1)}, u32[]{:S(2)}, u32[]{:S(2)}) async-start(bf16[4,256,512]{1,2,0:T(8,128)(2,1)} %broadcast_in_dim.14), calls=%async_computation | async-start | bytes 2097152 | tf_op jit(solution)/shard_map/all_to_all | solution.py:48
  19.2 18.0 %reduce-window.6 = s32[64,8,128]{2,1,0:T(8,128)S(1)} reduce-window(s32[64,8,128]{2,1,0:T(8,128)S(1)} %fusion.47, s32[]{:T(128)} %constant.62.clone.1), window={size=1x1x128 pad=0_0x0_0x127_0}, to_apply=%region_6.7 | reduce-window | flops 8323072 | bytes 524292 | tf_op jit(solution)/shard_map/reduce-window
  37.4 0.1 copy.91
  37.7 0.1 broadcast_add_fusion
  38.1 2.5 fusion.7
  40.7 1.6 multiply_reduce_fusion.1
  42.3 1.6 fusion.32
  43.9 5.8 %convolution_convert_fusion = bf16[2048,2048]{1,0:T(8,128)(2,1)} fusion(bf16[2048,256]{1,0:T(8,128)(2,1)S(1)} %copy-done.4, bf16[256,2048]{0,1:T(8,128)(2,1)S(1)} %fusion.32), kind=kOutput, calls=%fused_computation.4 | convolution fusion | flops 2151677952 | bytes 10485760 | tf_op jit(solution)/shard_map/dot_general | solution.py:143
  49.7 10.8 %all-to-all-start.3 = ((bf16[64,1,32,2048]{3,2,1,0:T(8,128)(2,1)}), bf16[64,1,32,2048]{3,2,1,0:T(8,128)(2,1)}, u32[]{:S(2)}, u32[]{:S(2)}) async-start(bf16[64,1,32,2048]{3,2,1,0:T(8,128)(2,1)} %bitcast.150), calls=%async_computation.3 | async-start | bytes 16777216 | tf_op jit(solution)/shard_map/all_to_all | solution.py:148
  60.5 0.2 all-gather.5.cloned.1.call-start
  60.7 0.5 all-gather.5.cloned.1.call-update
  61.3 3.9 fusion.60
  65.1 6.7 %convolution_convert_fusion.1 = bf16[256,2048]{1,0:T(8,128)(2,1)} fusion(bf16[704,2048]{1,0:T(8,128)(2,1)S(1)} %copy-done, bf16[2048,704]{0,1:T(8,128)(2,1)} %param.20, bf16[256,2048]{0,1:T(8,128)(2,1)} %copy-done.2, f32[256,704]{0,1:T(8,128)} %fusion.60), kind=kOutput, calls=%fused_computation.20 | convolution fusion | flops 1478000640 | bytes 8585216 | tf_op jit(solution)/shard_map/dot_general | solution.py:158
  71.8 2.3 copy.116
  74.1 1.1 fusion.45
  75.3 50.4 %all-gather.3.cloned.1.call-done = bf16[1408,4096]{1,0:T(8,128)(2,1)} async-done(((bf16[352,4096]{1,0:T(8,128)(2,1)}), bf16[1408,4096]{1,0:T(8,128)(2,1)}) %all-gather.3.cloned.1.call-update) | async-done | bytes 11534352 | tf_op jit(solution)/shard_map/all_gather | solution.py:64
  125.7 11.0 %fusion.58 = (bf16[1408,2048]{1,0:T(8,128)(2,1)}, bf16[1408,2048]{1,0:T(8,128)(2,1)}) fusion(bf16[1408,4096]{1,0:T(8,128)(2,1)} %all-gather.3.cloned.1.call-done), kind=kLoop, calls=%fused_computation.78 | loop fusion | bytes 23068672 | tf_op jit(solution)/shard_map/slice | solution.py:66
  136.6 8.5 %copy.102 = bf16[1408,2048]{0,1:T(8,128)(2,1)} copy(bf16[1408,2048]{1,0:T(8,128)(2,1)} %get-tuple-element.7) | data formatting | bytes 11534336
  145.2 8.4 %copy.103 = bf16[1408,2048]{0,1:T(8,128)(2,1)} copy(bf16[1408,2048]{1,0:T(8,128)(2,1)} %get-tuple-element.8) | data formatting | bytes 11534336
  153.5 93.1 %all-to-all-done.3 = bf16[64,1,32,2048]{3,2,1,0:T(8,128)(2,1)} async-done(((bf16[64,1,32,2048]{3,2,1,0:T(8,128)(2,1)}), bf16[64,1,32,2048]{3,2,1,0:T(8,128)(2,1)}, u32[]{:S(2)}, u32[]{:S(2)}) %all-to-all-start.3) | async-done | bytes 8388640 | tf_op jit(solution)/shard_map/all_to_all | solution.py:148
  246.6 0.7 broadcast_in_dim.15
  247.3 4.8 %all-to-all-start.2 = ((f32[4,256,60]{1,2,0:T(8,128)}), f32[4,256,60]{1,2,0:T(8,128)S(1)}, u32[]{:S(2)}, u32[]{:S(2)}) async-start(f32[4,256,60]{1,2,0:T(8,128)} %broadcast_in_dim.15), calls=%async_computation.2 | async-start | bytes 524288 | tf_op jit(solution)/shard_map/all_to_all | solution.py:48
  252.2 8.3 %fusion.8 = f32[16,1,32,1408]{3,2,0,1:T(8,128)} fusion(bf16[1408,2048]{0,1:T(8,128)(2,1)} %copy.102, bf16[64,1,32,2048]{3,2,1,0:T(8,128)(2,1)} %all-to-all-done.3, s32[]{:T(128)S(6)} %select_n.65), kind=kOutput, calls=%fused_computation.12 | convolution fusion | flops 2952790016 | bytes 10747908 | tf_op jit(solution)/shard_map/sekd,edf->sekf/dot_general | solution.py:90
  260.5 14.1 %fusion.23 = bf16[16,1,32,2048]{3,2,0,1:T(8,128)(2,1)} fusion(bf16[1,1408,2048]{2,1,0:T(8,128)(2,1)} %all-gather.5.cloned.1.call-done, bf16[1408,2048]{0,1:T(8,128)(2,1)} %copy.103, f32[16,1,32,1408]{3,2,0,1:T(8,128)} %fusion.8, bf16[64,1,32,2048]{3,2,1,0:T(8,128)(2,1)} %all-to-all-done.3, s32[]{:T(128)S(6)} %select_n.65), kind=kOutput, calls=%fused_computation.18 | convolution fusion | flops 5910953984 | bytes 18612228 | tf_op jit(solution)/shard_map/sekf,efd->sekd/dot_general | solution.py:93
  274.6 3.3 reshape.185
  277.9 4.8 %all-to-all-start.1 = ((bf16[4,256,512]{2,1,0:T(8,128)(2,1)}), bf16[4,256,512]{2,1,0:T(8,128)(2,1)}, u32[]{:S(2)}, u32[]{:S(2)}) async-start(bf16[4,256,512]{2,1,0:T(8,128)(2,1)} %bitcast.152), calls=%async_computation.1 | async-start | bytes 2097152 | tf_op jit(solution)/shard_map/all_to_all | solution.py:79
  282.7 4.4 %constant_dynamic-slice_fusion.3 = (bf16[16,1,32,1,512]{4,3,2,0,1:T(2,128)(2,1)S(1)}, bf16[16,1,32,1,512]{4,3,2,0,1:T(2,128)(2,1)S(1)}, bf16[16,1,32,1,512]{4,3,...) fusion(bf16[16,1,32,4,512]{4,3,2,0,1:T(4,128)(2,1)S(1)} %reshape.185, s32[]{:T(128)S(6)} %select_n.66, s32[]{:T(128)S(6)} %select_n.70, ...), kind=kLoop, calls=%fused_computation.68 | loop fusion | bytes 4194320 | tf_op jit(solution)/shard_map/dynamic-slice
  287.3 1.5 collective-permute-start
  288.9 1.0 collective-permute-start.1
  290.1 2.7 collective-permute-start.2
  292.8 0.1 copy.120
  292.9 19.1 %collective-permute-done = bf16[16,1,32,512]{3,2,0,1:T(8,128)(2,1)S(1)} collective-permute-done((bf16[16,1,32,512]{3,2,0,1:T(8,128)(2,1)S(1)}, bf16[16,1,32,512]{3,2,0,1:T(8,128)(2,1)S(1)}, u32[]{:S(2)}, u32[]{:S(2)}) %collective-permute-start) | collective-permute-done | bytes 524320 | tf_op jit(solution)/shard_map/ppermute | solution.py:28
  312.1 2.4 collective-permute-done.2
  314.5 0.3 maximum_bitcast_fusion
  314.8 2.0 gather_fusion
  316.8 10.2 %all-to-all-start.4 = ((bf16[64,1,32,512]{3,2,1,0:T(8,128)(2,1)}), bf16[64,1,32,512]{3,2,1,0:T(8,128)(2,1)}, u32[]{:S(2)}, u32[]{:S(2)}) async-start(bf16[64,1,32,512]{3,2,1,0:T(8,128)(2,1)} %bitcast.151), calls=%async_computation.4 | async-start | bytes 4194304 | tf_op jit(solution)/shard_map/all_to_all | solution.py:84
  327.0 0.1 copy.101
  327.3 0.2 fusion.59
  327.8 0.1 copy.87
  327.9 1.5 convert_reduce_fusion
  329.4 48.8 %all-to-all-done.4 = bf16[64,1,32,512]{3,2,1,0:T(8,128)(2,1)} async-done(((bf16[64,1,32,512]{3,2,1,0:T(8,128)(2,1)}), bf16[64,1,32,512]{3,2,1,0:T(8,128)(2,1)}, u32[]{:S(2)}, u32[]{:S(2)}) %all-to-all-start.4) | async-done | bytes 2097184 | tf_op jit(solution)/shard_map/all_to_all | solution.py:84
  378.2 7.1 %gather_fusion.1 = bf16[1024,512]{1,0:T(8,128)(2,1)} fusion(bf16[2048,512]{1,0:T(8,128)(2,1)} %bitcast.43, s32[1024]{0:T(1024)S(1)} %broadcast_clamp_fusion), kind=kCustom, calls=%fused_computation.1 | custom fusion | bytes 2101248 | tf_op jit(solution)/shard_map/gather | solution.py:153
  385.3 2.8 reshape.210
  388.0 3.0 multiply_reduce_fusion
  391.0 0.8 add_convert_fusion
  (54 shorter events, 1.9 us)
Async XLA Ops:
  6.5 58.6 %copy-start = (bf16[704,2048]{1,0:T(8,128)(2,1)S(1)}, bf16[704,2048]{1,0:T(8,128)(2,1)}, u32[]{:S(2)}) copy-start(bf16[704,2048]{1,0:T(8,128)(2,1)} %param.21) | copy-start | bytes 8650756
  6.5 119.1 %all-gather.3.cloned.1.call-start = ((), (), s32[]{:S(2)}) async-start(), calls=%async_computation.5 | async-start | bytes 14417920 | tf_op jit(solution)/shard_map/all_gather | solution.py:64
  10.3 0.9 copy-start.5
  10.4 8.5 %copy-start.7 = (s32[256,4]{0,1:T(4,128)S(1)}, s32[256,4]{0,1:T(4,128)}, u32[]{:S(2)}) copy-start(s32[256,4]{0,1:T(4,128)} %param.15) | copy-start | bytes 12292
  12.5 28.2 %all-to-all-start = ((bf16[4,256,512]{1,2,0:T(8,128)(2,1)}), bf16[4,256,512]{1,2,0:T(8,128)(2,1)}, u32[]{:S(2)}, u32[]{:S(2)}) async-start(bf16[4,256,512]{1,2,0:T(8,128)(2,1)} %broadcast_in_dim.14), calls=%async_computation | async-start | bytes 2097152 | tf_op jit(solution)/shard_map/all_to_all | solution.py:48
  18.8 23.5 %copy-start.8 = (f32[2048]{0:T(1024)S(1)}, f32[2048]{0:T(1024)}, u32[]{:S(2)}) copy-start(f32[2048]{0:T(1024)} %param.12) | copy-start | bytes 24580
  40.7 3.2 copy-start.4
  43.9 5.8 %copy-start.2 = (bf16[256,2048]{0,1:T(8,128)(2,1)}, bf16[256,2048]{0,1:T(8,128)(2,1)S(1)}, u32[]{:S(2)}) copy-start(bf16[256,2048]{0,1:T(8,128)(2,1)S(1)} %fusion.32) | copy-start | bytes 3145732
  49.7 196.9 %all-to-all-start.3 = ((bf16[64,1,32,2048]{3,2,1,0:T(8,128)(2,1)}), bf16[64,1,32,2048]{3,2,1,0:T(8,128)(2,1)}, u32[]{:S(2)}, u32[]{:S(2)}) async-start(bf16[64,1,32,2048]{3,2,1,0:T(8,128)(2,1)} %bitcast.150), calls=%async_computation.3 | async-start | bytes 16777216 | tf_op jit(solution)/shard_map/all_to_all | solution.py:148
  60.5 200.0 %all-gather.5.cloned.1.call-start = ((), (), s32[]{:S(2)}) async-start(), calls=%async_computation.6 | async-start | bytes 7208960 | tf_op jit(solution)/shard_map/all_gather | solution.py:128
  65.1 9.0 %copy-start.6 = (bf16[512,60]{0,1:T(8,128)(2,1)S(1)}, bf16[512,60]{0,1:T(8,128)(2,1)}, u32[]{:S(2)}) copy-start(bf16[512,60]{0,1:T(8,128)(2,1)} %param.13) | copy-start | bytes 184324
  247.3 30.5 %all-to-all-start.2 = ((f32[4,256,60]{1,2,0:T(8,128)}), f32[4,256,60]{1,2,0:T(8,128)S(1)}, u32[]{:S(2)}, u32[]{:S(2)}) async-start(f32[4,256,60]{1,2,0:T(8,128)} %broadcast_in_dim.15), calls=%async_computation.2 | async-start | bytes 524288 | tf_op jit(solution)/shard_map/all_to_all | solution.py:48
  277.9 38.9 %all-to-all-start.1 = ((bf16[4,256,512]{2,1,0:T(8,128)(2,1)}), bf16[4,256,512]{2,1,0:T(8,128)(2,1)}, u32[]{:S(2)}, u32[]{:S(2)}) async-start(bf16[4,256,512]{2,1,0:T(8,128)(2,1)} %bitcast.152), calls=%async_computation.1 | async-start | bytes 2097152 | tf_op jit(solution)/shard_map/all_to_all | solution.py:79
  287.3 24.8 %collective-permute-start = (bf16[16,1,32,512]{3,2,0,1:T(8,128)(2,1)S(1)}, bf16[16,1,32,512]{3,2,0,1:T(8,128)(2,1)S(1)}, u32[]{:S(2)}, u32[]{:S(2)}) collective-permute-start(bf16[16,1,32,512]{3,2,0,1:T(8,128)(2,1)S(1)} %bitcast.158), channel_id=1, source_target_pairs={{0,1},{1,2},{2,3},{3,0},{4,5},{5,6},{6,7},{7,4},{8,9},{9,10},{10,1... | collective-permute-start | bytes 1572872 | tf_op jit(solution)/shard_map/ppermute | solution.py:28
  288.9 23.1 %collective-permute-start.1 = (bf16[16,1,32,512]{3,2,0,1:T(8,128)(2,1)S(1)}, bf16[16,1,32,512]{3,2,0,1:T(8,128)(2,1)S(1)}, u32[]{:S(2)}, u32[]{:S(2)}) collective-permute-start(bf16[16,1,32,512]{3,2,0,1:T(8,128)(2,1)S(1)} %bitcast.159), channel_id=1, source_target_pairs={{0,2},{1,3},{2,0},{3,1},{4,6},{5,7},{6,4},{7,5},{8,10},{9,11},{10,... | collective-permute-start | bytes 1572872 | tf_op jit(solution)/shard_map/ppermute | solution.py:28
  290.1 24.4 %collective-permute-start.2 = (bf16[16,1,32,512]{3,2,0,1:T(8,128)(2,1)S(1)}, bf16[16,1,32,512]{3,2,0,1:T(8,128)(2,1)S(1)}, u32[]{:S(2)}, u32[]{:S(2)}) collective-permute-start(bf16[16,1,32,512]{3,2,0,1:T(8,128)(2,1)S(1)} %bitcast.160), channel_id=1, source_target_pairs={{0,3},{1,0},{2,1},{3,2},{4,7},{5,4},{6,5},{7,6},{8,11},{9,8},{10,9... | collective-permute-start | bytes 1572872 | tf_op jit(solution)/shard_map/ppermute | solution.py:28
  316.7 10.5 %copy-start.9 = (bf16[2048]{0:T(1024)(128)(2,1)S(1)}, bf16[2048]{0:T(1024)(128)(2,1)}, u32[]{:S(2)}) copy-start(bf16[2048]{0:T(1024)(128)(2,1)} %param.14) | copy-start | bytes 12292
  316.7 10.6 %copy-start.3 = (bf16[256,2048]{0,1:T(8,128)(2,1)S(1)}, bf16[256,2048]{0,1:T(8,128)(2,1)}, u32[]{:S(2)}) copy-start(bf16[256,2048]{0,1:T(8,128)(2,1)} %copy-done.2) | copy-start | bytes 3145732
  316.8 61.4 %all-to-all-start.4 = ((bf16[64,1,32,512]{3,2,1,0:T(8,128)(2,1)}), bf16[64,1,32,512]{3,2,1,0:T(8,128)(2,1)}, u32[]{:S(2)}, u32[]{:S(2)}) async-start(bf16[64,1,32,512]{3,2,1,0:T(8,128)(2,1)} %bitcast.151), calls=%async_computation.4 | async-start | bytes 4194304 | tf_op jit(solution)/shard_map/all_to_all | solution.py:84
  378.2 13.7 %copy-start.1 = (bf16[704,2048]{1,0:T(8,128)(2,1)S(1)}, bf16[704,2048]{1,0:T(8,128)(2,1)}, u32[]{:S(2)}) copy-start(bf16[704,2048]{1,0:T(8,128)(2,1)} %param.21) | copy-start | bytes 8650756
Sparse Core Ops, SparseCore 0:
  10.5 115.1 all-gather.2
  127.5 64.4 all-gather.4
